TPU v7x, 256 devices: a 4x2x16 block of a 4x16x16 slice. The times are simulated.
256 devices in a mesh: groups: 2 (over y), blk: 128 (over z, x, core).
Axes of the slice: x: 4, y: 2, z: 16, core: 2. Of those that a mesh axis runs over, the one named last changes fastest.
The devices are a block of a 4x16x16 slice.
Arguments:
- positions: float32 [3, 65536], P(None, ('groups', 'blk')), parts along dimension 1, may hold values from 0 to 96
- right_side: float32 [3, 65536], P(None, ('groups', 'blk')), parts along dimension 1, may hold values from -18 to 18
- neighbours: int32 [16, 65536], P(None, ('groups', 'blk')), parts along dimension 1, may hold values from 0 to 32767, as said below
- counts: int32 [65536], P(('groups', 'blk')), parts along dimension 0, may hold values from 1 to 16
Outputs:
- solution: float32 [3, 65536], P(None, ('groups', 'blk')), parts along dimension 1
- residual: float32 [3, 65536], P(None, ('groups', 'blk')), parts along dimension 1
There are 2 independent parts, one for each index of `groups`. A program takes and returns all parts, laid end to end along the dimension named above; each array names one. Nothing has to cross between parts.
Inputs may be any that keep to these rules, and one draw needn't show every extreme that they name: `neighbours`: every entry in column i lies within 32 of i, counted cyclically over the 32768 particles.
All inputs are finite; a program needn't handle non-finite values.
Results may differ from a plain program's by a relative error of at most 0.0003.
Values sent between devices are 32-bit elements; how exact they have to be, the bound alone decides.
A program may use at most 64 MiB of HBM per device.

v0:
```python
import functools
import math
import jax
import jax.numpy as jnp
from jax import lax
from jax.sharding import Mesh
from jax.sharding import PartitionSpec as P

REACH = 32
ITERS = 2
BLK = ("blk_0", "blk_1", "blk_2")
GROUPS_BLK = ("groups", "blk_0", "blk_1", "blk_2")
SOFT = 0.0001
EPS = 1e-06


def extended_2(cells, sides, width):
    for axis, dim in sides:
        count = lax.axis_size(axis)
        head = lax.slice_in_dim(cells, 0, width, axis=dim)
        tail = lax.slice_in_dim(cells, cells.shape[dim] - width, cells.shape[dim], axis=dim)
        cells = jnp.concatenate(
            [
                lax.ppermute(tail, axis, [(i, (i + 1) % count) for i in range(count)]),
                cells,
                lax.ppermute(head, axis, [((i + 1) % count, i) for i in range(count)]),
            ],
            axis=dim,
        )
    return cells


def joined_along(tiles, dim):
    lengths = list(tiles.shape[1:])
    lengths[dim] *= tiles.shape[0]
    return jnp.moveaxis(tiles, 0, dim).reshape(lengths)


def stacked_from(array, axes, turns):
    tiles = array[None]
    for k in turns:
        tiles = lax.all_gather(tiles, axes[k], axis=0, tiled=True)
    held = [lax.axis_size(axes[k]) for k in reversed(turns)]
    tiles = tiles.reshape(*held, *array.shape)
    turned = sorted(range(len(turns)), key=lambda place: turns[len(turns) - 1 - place])
    return tiles.transpose(*turned, *range(len(turns), tiles.ndim)).reshape(-1, *array.shape)


def gathered_by_axis(array, axes, turns, dim):
    return joined_along(stacked_from(array, axes, turns), dim)


def one_axis_at_a_time(array, axes):
    return functools.reduce(lax.psum, axes, array)


def pair_coefficients(dx, dy, dz):
    dist = jnp.sqrt(dx * dx + dy * dy + dz * dz + SOFT)
    inverse = 1.0 / dist
    cube = inverse * inverse * inverse
    correlation = dist < 2.0
    coef_a = jnp.where(correlation, 1.0 - 9.0 * dist / 32.0, 0.75 * inverse + 0.5 * cube)
    coef_b = jnp.where(
        correlation, 3.0 / 32.0 * inverse, 0.75 * cube - 1.5 * cube * inverse * inverse
    )
    return (coef_a, coef_b)


def far_tile(row_pos, col_pos, col_vec):
    dx = row_pos[0][:, None] - col_pos[0][None, :]
    dy = row_pos[1][:, None] - col_pos[1][None, :]
    dz = row_pos[2][:, None] - col_pos[2][None, :]
    coef_a, coef_b = pair_coefficients(dx, dy, dz)
    along = dx * col_vec[0][None, :] + dy * col_vec[1][None, :] + dz * col_vec[2][None, :]
    weighted = coef_b * along
    out_x = jnp.sum(coef_a * col_vec[0][None, :] + weighted * dx, axis=1)
    out_y = jnp.sum(coef_a * col_vec[1][None, :] + weighted * dy, axis=1)
    out_z = jnp.sum(coef_a * col_vec[2][None, :] + weighted * dz, axis=1)
    return jnp.stack([out_x, out_y, out_z])


def far_piece(row_pos, col_pos, col_vec):
    width = col_pos.shape[1]
    size = math.gcd(width, 4096)
    count = width // size
    stacked_pos = col_pos.reshape(3, count, size).transpose(1, 0, 2)
    stacked_vec = col_vec.reshape(3, count, size).transpose(1, 0, 2)

    def advance(carry, item):
        return (carry + far_tile(row_pos, item[0], item[1]), None)

    start_sum = jnp.zeros((3, row_pos.shape[1]), jnp.float32)
    result, unused = lax.scan(advance, start_sum, (stacked_pos, stacked_vec))
    return result


def lubrication(positions, vec, near_pos, near_vec, live):
    delta = positions[:, None, :] - near_pos
    square = jnp.sum(delta * delta, axis=0) + SOFT
    dist = jnp.sqrt(square)
    strength = live / ((0.5 + jnp.abs(dist - 2.0)) * square)
    along = jnp.sum(delta * (vec[:, None, :] - near_vec), axis=0)
    return jnp.sum(delta * (strength * along)[None], axis=1)


def on_device(positions, right_side, neighbours, counts):
    rows = positions.shape[1]
    blocks = lax.axis_size(BLK)
    total = rows * blocks
    first_row = lax.axis_index(BLK) * rows
    slots = jnp.arange(neighbours.shape[0], dtype=jnp.int32)
    live = (slots[:, None] < counts[None, :]).astype(jnp.float32)
    local_slot = jnp.remainder(neighbours - first_row + REACH, total)
    beta = jnp.sqrt(one_axis_at_a_time(jnp.sum(right_side * right_side), BLK) + EPS)
    basis = [right_side / beta]
    images = []
    cosines = []
    sines = []
    rotated = [beta]
    columns = []
    for step in range(ITERS):
        vec = basis[step]
        stacked = jnp.concatenate([positions, vec], axis=0)
        extended = extended_2(stacked, ((BLK, 1),), REACH)
        picked = jnp.take(extended, local_slot, axis=1)
        gathered = gathered_by_axis(stacked, BLK, (1, 0, 2), 1)
        far = far_piece(positions, gathered[:3], gathered[3:])
        work = far + lubrication(positions, vec, picked[:3], picked[3:], live)
        images.append(work)
        local_terms = tuple((jnp.sum(work * basis[j]) for j in range(step + 1))) + (
            jnp.sum(work * work),
        )
        totals = jax.tree.map(lambda part: one_axis_at_a_time(part, BLK), local_terms)
        column = list(totals[: step + 1])
        squares = totals[step + 1]
        for j in range(step + 1):
            work = work - column[j] * basis[j]
            squares = squares - column[j] * column[j]
        below = jnp.sqrt(squares + EPS)
        basis.append(work / below)
        column.append(below)
        for j in range(step):
            first, second = (column[j], column[j + 1])
            column[j] = cosines[j] * first + sines[j] * second
            column[j + 1] = -sines[j] * first + cosines[j] * second
        pivot = jnp.sqrt(column[step] * column[step] + below * below)
        cosines.append(column[step] / pivot)
        sines.append(below / pivot)
        column[step] = pivot
        rotated.append(-sines[step] * rotated[step])
        rotated[step] = cosines[step] * rotated[step]
        columns.append(column)
    coeffs = [None] * ITERS
    for step in reversed(range(ITERS)):
        accum = rotated[step]
        for j in range(step + 1, ITERS):
            accum = accum - columns[j][step] * coeffs[j]
        coeffs[step] = accum / columns[step][step]
    solution = jnp.zeros_like(right_side)
    residual = right_side
    for step in range(ITERS):
        solution = solution + coeffs[step] * basis[step]
        residual = residual - coeffs[step] * images[step]
    return (solution, residual)


def solution(mesh):
    torus = Mesh(
        mesh.devices.reshape(mesh.shape["groups"], 16, 4, 2), ("groups", "blk_0", "blk_1", "blk_2")
    )
    placed = (P(None, GROUPS_BLK), P(None, GROUPS_BLK), P(None, GROUPS_BLK), P(GROUPS_BLK))
    return jax.shard_map(
        on_device,
        mesh=torus,
        in_specs=placed,
        out_specs=(P(None, GROUPS_BLK), P(None, GROUPS_BLK)),
        check_vma=False,
    )
```

profile of v0, /device:TPU:33, one launch (start us, length us, event | category | flops | bytes accessed | tf_op | source)
XLA Modules:
  0.0 429.3 jit_solution(15191888906879357911)
XLA Ops:
  0.6 1.3 multiply_reduce_fusion.9
  1.9 43.8 %psum.126 = f32[]{:T(128)} all-reduce(f32[]{:T(128)} %multiply_reduce_fusion.9), channel_id=1, replica_groups=mesh['groups'=2,'blk_0'=16,'blk_1'=4,'blk_2'=2] {'blk_0'}, use_global_device_ids=true, to_apply=%region_1.2 | all-reduce | flops 1 | bytes 8 | tf_op jit(solution)/shard_map/psum | solution.py:54
  45.7 9.5 %psum.127 = f32[]{:T(128)} all-reduce(f32[]{:T(128)} %psum.126), channel_id=1, replica_groups=mesh['groups'=2,'blk_0'=16,'blk_1'=4,'blk_2'=2] {'blk_1'}, use_global_device_ids=true, to_apply=%region_2.3 | all-reduce | flops 1 | bytes 8 | tf_op jit(solution)/shard_map/psum | solution.py:54
  55.2 12.4 %psum.128 = f32[]{:T(128)} all-reduce(f32[]{:T(128)} %psum.127), channel_id=1, replica_groups=mesh['groups'=2,'blk_0'=16,'blk_1'=4,'blk_2'=2] {'blk_2'}, use_global_device_ids=true, to_apply=%region_3.4 | all-reduce | flops 1 | bytes 8 | tf_op jit(solution)/shard_map/psum | solution.py:54
  68.4 0.7 broadcast_divide_fusion
  69.0 0.8 fusion.55
  69.9 0.5 collective-permute-start.1
  70.4 0.7 fusion.51
  71.1 0.7 fusion.57
  71.8 9.1 %all-gather.2 = f32[4,6,256]{2,1,0:T(8,128)S(1)} all-gather(f32[1,6,256]{2,1,0:T(8,128)S(1)} %fusion.51), channel_id=2, replica_groups=mesh['groups'=2,'blk_0'=16,'blk_1'=4,'blk_2'=2] {'blk_1'}, dimensions={0}, use_global_device_ids=true | all-gather | bytes 30720 | tf_op jit(solution)/shard_map/all_gather | solution.py:42
  80.9 24.3 %all_gather.19 = f32[64,6,256]{2,1,0:T(8,128)S(1)} all-gather(f32[4,6,256]{2,1,0:T(8,128)S(1)} %all-gather.2), channel_id=1, replica_groups=mesh['groups'=2,'blk_0'=16,'blk_1'=4,'blk_2'=2] {'blk_0'}, dimensions={0}, use_global_device_ids=true | all-gather | bytes 417792 | tf_op jit(solution)/shard_map/all_gather | solution.py:42
  105.4 14.5 %all_gather.20 = f32[128,6,256]{2,0,1:T(8,128)S(1)} all-gather(f32[64,6,256]{2,0,1:T(8,128)S(1)} %copy.85), channel_id=1, replica_groups=mesh['groups'=2,'blk_0'=16,'blk_1'=4,'blk_2'=2] {'blk_2'}, dimensions={0}, use_global_device_ids=true | all-gather | bytes 1179648 | tf_op jit(solution)/shard_map/all_gather | solution.py:42
  119.9 0.2 reshape.139
  120.1 0.6 copy.108
  120.7 0.5 reshape.140
  121.5 0.5 copy_bitcast_fusion.4
  122.1 66.1 %while.26 = (s32[]{:T(128)}, f32[3,256]{1,0:T(4,128)S(1)}, f32[3,256]{1,0:T(4,128)S(1)}, f32[8,3,4096]{2,1,0:T(4,128)S(1)}, f32[8,3,4096]{2,1,0:T(4,128)S(1)}, /*index=5*/s32[]{:T(128)}, s32[]{:T(128)}, s32[]{}, s32[]{}) while((s32[]{:T(128)}, f32[3,256]{1,0:T(4,128)S(1)}, f32[3,256]{1,0:T(4,128)S(1)}, ...), condition=%wide.region_8.9_spmd.clone, body=%wide.region_4.0_spmd.clone.sunk | while | flops 46139652 | bytes 316555 | solution.py:93
  122.2 8.1 %fusion.67 = (f32[256]{0:T(256)S(1)}, f32[256]{0:T(256)S(1)}, f32[256]{0:T(256)S(1)}) fusion(f32[4096]{0:T(1024)S(1)} %bitcast.120, f32[4096]{0:T(1024)S(1)} %bitcast.123, f32[256]{0:T(256)S(1)} %bitcast.140, f32[4096]{0:T(1024)S(1)} %bitcast.122, f32[256]{0:T(256)S(1)} %bitcast.139, f32[4096]{0:T(1024)S(1)} %bitcast.124, f32[256]{0:T(256)S(1)} %bitcast.138, ...), kind=kLoop, calls=%fused_computation.23.clone.1 | loop fusion | flops 46136576 | bytes 104448 | tf_op jit(solution)/shard_map/while/body/eval_jaxpr/reduce_sum | solution.py:76
  130.5 8.1 %fusion.67 = (f32[256]{0:T(256)S(1)}, f32[256]{0:T(256)S(1)}, f32[256]{0:T(256)S(1)}) fusion(f32[4096]{0:T(1024)S(1)} %bitcast.120, f32[4096]{0:T(1024)S(1)} %bitcast.123, f32[256]{0:T(256)S(1)} %bitcast.140, f32[4096]{0:T(1024)S(1)} %bitcast.122, f32[256]{0:T(256)S(1)} %bitcast.139, f32[4096]{0:T(1024)S(1)} %bitcast.124, f32[256]{0:T(256)S(1)} %bitcast.138, ...), kind=kLoop, calls=%fused_computation.23.clone.1 | loop fusion | flops 46136576 | bytes 104448 | tf_op jit(solution)/shard_map/while/body/eval_jaxpr/reduce_sum | solution.py:76
  138.7 8.1 %fusion.67 = (f32[256]{0:T(256)S(1)}, f32[256]{0:T(256)S(1)}, f32[256]{0:T(256)S(1)}) fusion(f32[4096]{0:T(1024)S(1)} %bitcast.120, f32[4096]{0:T(1024)S(1)} %bitcast.123, f32[256]{0:T(256)S(1)} %bitcast.140, f32[4096]{0:T(1024)S(1)} %bitcast.122, f32[256]{0:T(256)S(1)} %bitcast.139, f32[4096]{0:T(1024)S(1)} %bitcast.124, f32[256]{0:T(256)S(1)} %bitcast.138, ...), kind=kLoop, calls=%fused_computation.23.clone.1 | loop fusion | flops 46136576 | bytes 104448 | tf_op jit(solution)/shard_map/while/body/eval_jaxpr/reduce_sum | solution.py:76
  147.0 8.1 %fusion.67 = (f32[256]{0:T(256)S(1)}, f32[256]{0:T(256)S(1)}, f32[256]{0:T(256)S(1)}) fusion(f32[4096]{0:T(1024)S(1)} %bitcast.120, f32[4096]{0:T(1024)S(1)} %bitcast.123, f32[256]{0:T(256)S(1)} %bitcast.140, f32[4096]{0:T(1024)S(1)} %bitcast.122, f32[256]{0:T(256)S(1)} %bitcast.139, f32[4096]{0:T(1024)S(1)} %bitcast.124, f32[256]{0:T(256)S(1)} %bitcast.138, ...), kind=kLoop, calls=%fused_computation.23.clone.1 | loop fusion | flops 46136576 | bytes 104448 | tf_op jit(solution)/shard_map/while/body/eval_jaxpr/reduce_sum | solution.py:76
  155.3 8.1 %fusion.67 = (f32[256]{0:T(256)S(1)}, f32[256]{0:T(256)S(1)}, f32[256]{0:T(256)S(1)}) fusion(f32[4096]{0:T(1024)S(1)} %bitcast.120, f32[4096]{0:T(1024)S(1)} %bitcast.123, f32[256]{0:T(256)S(1)} %bitcast.140, f32[4096]{0:T(1024)S(1)} %bitcast.122, f32[256]{0:T(256)S(1)} %bitcast.139, f32[4096]{0:T(1024)S(1)} %bitcast.124, f32[256]{0:T(256)S(1)} %bitcast.138, ...), kind=kLoop, calls=%fused_computation.23.clone.1 | loop fusion | flops 46136576 | bytes 104448 | tf_op jit(solution)/shard_map/while/body/eval_jaxpr/reduce_sum | solution.py:76
  163.5 8.1 %fusion.67 = (f32[256]{0:T(256)S(1)}, f32[256]{0:T(256)S(1)}, f32[256]{0:T(256)S(1)}) fusion(f32[4096]{0:T(1024)S(1)} %bitcast.120, f32[4096]{0:T(1024)S(1)} %bitcast.123, f32[256]{0:T(256)S(1)} %bitcast.140, f32[4096]{0:T(1024)S(1)} %bitcast.122, f32[256]{0:T(256)S(1)} %bitcast.139, f32[4096]{0:T(1024)S(1)} %bitcast.124, f32[256]{0:T(256)S(1)} %bitcast.138, ...), kind=kLoop, calls=%fused_computation.23.clone.1 | loop fusion | flops 46136576 | bytes 104448 | tf_op jit(solution)/shard_map/while/body/eval_jaxpr/reduce_sum | solution.py:76
  171.8 8.1 %fusion.67 = (f32[256]{0:T(256)S(1)}, f32[256]{0:T(256)S(1)}, f32[256]{0:T(256)S(1)}) fusion(f32[4096]{0:T(1024)S(1)} %bitcast.120, f32[4096]{0:T(1024)S(1)} %bitcast.123, f32[256]{0:T(256)S(1)} %bitcast.140, f32[4096]{0:T(1024)S(1)} %bitcast.122, f32[256]{0:T(256)S(1)} %bitcast.139, f32[4096]{0:T(1024)S(1)} %bitcast.124, f32[256]{0:T(256)S(1)} %bitcast.138, ...), kind=kLoop, calls=%fused_computation.23.clone.1 | loop fusion | flops 46136576 | bytes 104448 | tf_op jit(solution)/shard_map/while/body/eval_jaxpr/reduce_sum | solution.py:76
  180.1 8.1 %fusion.67 = (f32[256]{0:T(256)S(1)}, f32[256]{0:T(256)S(1)}, f32[256]{0:T(256)S(1)}) fusion(f32[4096]{0:T(1024)S(1)} %bitcast.120, f32[4096]{0:T(1024)S(1)} %bitcast.123, f32[256]{0:T(256)S(1)} %bitcast.140, f32[4096]{0:T(1024)S(1)} %bitcast.122, f32[256]{0:T(256)S(1)} %bitcast.139, f32[4096]{0:T(1024)S(1)} %bitcast.124, f32[256]{0:T(256)S(1)} %bitcast.138, ...), kind=kLoop, calls=%fused_computation.23.clone.1 | loop fusion | flops 46136576 | bytes 104448 | tf_op jit(solution)/shard_map/while/body/eval_jaxpr/reduce_sum | solution.py:76
  188.6 0.1 copy.90
  188.8 10.8 %gather_fusion = f32[4096,6]{1,0:T(8,128)S(1)} fusion(f32[6,320]{0,1:T(8,128)S(1)} %copy.90, s32[4096]{0:T(1024)S(1)} %broadcast_clamp_fusion), kind=kCustom, calls=%fused_computation.clone | custom fusion | bytes 212992 | tf_op jit(solution)/shard_map/jit(_take)/gather | solution.py:125
  199.6 0.7 select_bitcast_fusion.1
  200.3 1.7 multiply_reduce_fusion.3
  202.1 0.7 multiply_reduce_fusion.2
  202.9 0.6 multiply_reduce_fusion.8
  203.5 22.6 %all-reduce.1 = (f32[]{:T(128)}, f32[]{:T(128)}) all-reduce(f32[]{:T(128)} %get-tuple-element.193, f32[]{:T(128)} %get-tuple-element.192), channel_id=1, replica_groups=mesh['groups'=2,'blk_0'=16,'blk_1'=4,'blk_2'=2] {'blk_0'}, use_global_device_ids=true, to_apply=%region_17.19 | all-reduce | flops 2 | bytes 16 | tf_op jit(solution)/shard_map/psum | solution.py:54
  226.1 7.0 %all-reduce.3 = (f32[]{:T(128)}, f32[]{:T(128)}) all-reduce(f32[]{:T(128)} %get-tuple-element.217, f32[]{:T(128)} %get-tuple-element.218), channel_id=1, replica_groups=mesh['groups'=2,'blk_0'=16,'blk_1'=4,'blk_2'=2] {'blk_1'}, use_global_device_ids=true, to_apply=%region_18.20 | all-reduce | flops 2 | bytes 16 | tf_op jit(solution)/shard_map/psum | solution.py:54
  233.0 11.8 %all-reduce.5 = (f32[]{:T(128)}, f32[]{:T(128)}) all-reduce(f32[]{:T(128)} %get-tuple-element.222, f32[]{:T(128)} %get-tuple-element.223), channel_id=1, replica_groups=mesh['groups'=2,'blk_0'=16,'blk_1'=4,'blk_2'=2] {'blk_2'}, use_global_device_ids=true, to_apply=%region_19.21 | all-reduce | flops 2 | bytes 16 | tf_op jit(solution)/shard_map/psum | solution.py:54
  246.8 0.7 subtract_divide_fusion
  247.6 1.9 collective-permute-start.2
  249.5 9.3 %all-gather.3 = f32[4,6,256]{2,1,0:T(8,128)S(1)} all-gather(f32[1,6,256]{2,1,0:T(8,128)S(1)} %fusion.52), channel_id=3, replica_groups=mesh['groups'=2,'blk_0'=16,'blk_1'=4,'blk_2'=2] {'blk_1'}, dimensions={0}, use_global_device_ids=true | all-gather | bytes 30720 | tf_op jit(solution)/shard_map/all_gather | solution.py:42
  258.7 23.0 %all_gather.22 = f32[64,6,256]{2,1,0:T(8,128)S(1)} all-gather(f32[4,6,256]{2,1,0:T(8,128)S(1)} %all-gather.3), channel_id=1, replica_groups=mesh['groups'=2,'blk_0'=16,'blk_1'=4,'blk_2'=2] {'blk_0'}, dimensions={0}, use_global_device_ids=true | all-gather | bytes 417792 | tf_op jit(solution)/shard_map/all_gather | solution.py:42
  281.9 14.6 %all_gather.23 = f32[128,6,256]{2,0,1:T(8,128)S(1)} all-gather(f32[64,6,256]{2,0,1:T(8,128)S(1)} %copy.93), channel_id=1, replica_groups=mesh['groups'=2,'blk_0'=16,'blk_1'=4,'blk_2'=2] {'blk_2'}, dimensions={0}, use_global_device_ids=true | all-gather | bytes 1179648 | tf_op jit(solution)/shard_map/all_gather | solution.py:42
  296.4 0.2 reshape.143
  296.7 0.6 copy.107
  297.3 0.5 reshape.144
  298.0 0.3 copy.109
  298.4 0.3 copy.110
  298.7 66.1 %while.27 = (s32[]{:T(128)}, f32[3,256]{1,0:T(4,128)S(1)}, f32[3,256]{1,0:T(4,128)S(1)}, f32[8,3,4096]{2,1,0:T(4,128)S(1)}, f32[8,3,4096]{2,1,0:T(4,128)S(1)}, /*index=5*/s32[]{:T(128)}, s32[]{:T(128)}, s32[]{}, s32[]{}) while((s32[]{:T(128)}, f32[3,256]{1,0:T(4,128)S(1)}, f32[3,256]{1,0:T(4,128)S(1)}, ...), condition=%wide.region_24.26_spmd.clone, body=%wide.region_20.25_spmd.clone.sunk | while | flops 46139652 | bytes 316555 | solution.py:93
  298.8 8.1 %fusion.69 = (f32[256]{0:T(256)S(1)}, f32[256]{0:T(256)S(1)}, f32[256]{0:T(256)S(1)}) fusion(f32[4096]{0:T(1024)S(1)} %bitcast.126, f32[4096]{0:T(1024)S(1)} %bitcast.129, f32[256]{0:T(256)S(1)} %bitcast.143, f32[4096]{0:T(1024)S(1)} %bitcast.128, f32[256]{0:T(256)S(1)} %bitcast.142, f32[4096]{0:T(1024)S(1)} %bitcast.130, f32[256]{0:T(256)S(1)} %bitcast.141, ...), kind=kLoop, calls=%fused_computation.61.clone.1 | loop fusion | flops 46136576 | bytes 104448 | tf_op jit(solution)/shard_map/while/body/eval_jaxpr/reduce_sum | solution.py:76
  307.0 8.1 %fusion.69 = (f32[256]{0:T(256)S(1)}, f32[256]{0:T(256)S(1)}, f32[256]{0:T(256)S(1)}) fusion(f32[4096]{0:T(1024)S(1)} %bitcast.126, f32[4096]{0:T(1024)S(1)} %bitcast.129, f32[256]{0:T(256)S(1)} %bitcast.143, f32[4096]{0:T(1024)S(1)} %bitcast.128, f32[256]{0:T(256)S(1)} %bitcast.142, f32[4096]{0:T(1024)S(1)} %bitcast.130, f32[256]{0:T(256)S(1)} %bitcast.141, ...), kind=kLoop, calls=%fused_computation.61.clone.1 | loop fusion | flops 46136576 | bytes 104448 | tf_op jit(solution)/shard_map/while/body/eval_jaxpr/reduce_sum | solution.py:76
  315.3 8.1 %fusion.69 = (f32[256]{0:T(256)S(1)}, f32[256]{0:T(256)S(1)}, f32[256]{0:T(256)S(1)}) fusion(f32[4096]{0:T(1024)S(1)} %bitcast.126, f32[4096]{0:T(1024)S(1)} %bitcast.129, f32[256]{0:T(256)S(1)} %bitcast.143, f32[4096]{0:T(1024)S(1)} %bitcast.128, f32[256]{0:T(256)S(1)} %bitcast.142, f32[4096]{0:T(1024)S(1)} %bitcast.130, f32[256]{0:T(256)S(1)} %bitcast.141, ...), kind=kLoop, calls=%fused_computation.61.clone.1 | loop fusion | flops 46136576 | bytes 104448 | tf_op jit(solution)/shard_map/while/body/eval_jaxpr/reduce_sum | solution.py:76
  323.6 8.1 %fusion.69 = (f32[256]{0:T(256)S(1)}, f32[256]{0:T(256)S(1)}, f32[256]{0:T(256)S(1)}) fusion(f32[4096]{0:T(1024)S(1)} %bitcast.126, f32[4096]{0:T(1024)S(1)} %bitcast.129, f32[256]{0:T(256)S(1)} %bitcast.143, f32[4096]{0:T(1024)S(1)} %bitcast.128, f32[256]{0:T(256)S(1)} %bitcast.142, f32[4096]{0:T(1024)S(1)} %bitcast.130, f32[256]{0:T(256)S(1)} %bitcast.141, ...), kind=kLoop, calls=%fused_computation.61.clone.1 | loop fusion | flops 46136576 | bytes 104448 | tf_op jit(solution)/shard_map/while/body/eval_jaxpr/reduce_sum | solution.py:76
  331.8 8.1 %fusion.69 = (f32[256]{0:T(256)S(1)}, f32[256]{0:T(256)S(1)}, f32[256]{0:T(256)S(1)}) fusion(f32[4096]{0:T(1024)S(1)} %bitcast.126, f32[4096]{0:T(1024)S(1)} %bitcast.129, f32[256]{0:T(256)S(1)} %bitcast.143, f32[4096]{0:T(1024)S(1)} %bitcast.128, f32[256]{0:T(256)S(1)} %bitcast.142, f32[4096]{0:T(1024)S(1)} %bitcast.130, f32[256]{0:T(256)S(1)} %bitcast.141, ...), kind=kLoop, calls=%fused_computation.61.clone.1 | loop fusion | flops 46136576 | bytes 104448 | tf_op jit(solution)/shard_map/while/body/eval_jaxpr/reduce_sum | solution.py:76
  340.1 8.1 %fusion.69 = (f32[256]{0:T(256)S(1)}, f32[256]{0:T(256)S(1)}, f32[256]{0:T(256)S(1)}) fusion(f32[4096]{0:T(1024)S(1)} %bitcast.126, f32[4096]{0:T(1024)S(1)} %bitcast.129, f32[256]{0:T(256)S(1)} %bitcast.143, f32[4096]{0:T(1024)S(1)} %bitcast.128, f32[256]{0:T(256)S(1)} %bitcast.142, f32[4096]{0:T(1024)S(1)} %bitcast.130, f32[256]{0:T(256)S(1)} %bitcast.141, ...), kind=kLoop, calls=%fused_computation.61.clone.1 | loop fusion | flops 46136576 | bytes 104448 | tf_op jit(solution)/shard_map/while/body/eval_jaxpr/reduce_sum | solution.py:76
  348.4 8.1 %fusion.69 = (f32[256]{0:T(256)S(1)}, f32[256]{0:T(256)S(1)}, f32[256]{0:T(256)S(1)}) fusion(f32[4096]{0:T(1024)S(1)} %bitcast.126, f32[4096]{0:T(1024)S(1)} %bitcast.129, f32[256]{0:T(256)S(1)} %bitcast.143, f32[4096]{0:T(1024)S(1)} %bitcast.128, f32[256]{0:T(256)S(1)} %bitcast.142, f32[4096]{0:T(1024)S(1)} %bitcast.130, f32[256]{0:T(256)S(1)} %bitcast.141, ...), kind=kLoop, calls=%fused_computation.61.clone.1 | loop fusion | flops 46136576 | bytes 104448 | tf_op jit(solution)/shard_map/while/body/eval_jaxpr/reduce_sum | solution.py:76
  356.6 8.1 %fusion.69 = (f32[256]{0:T(256)S(1)}, f32[256]{0:T(256)S(1)}, f32[256]{0:T(256)S(1)}) fusion(f32[4096]{0:T(1024)S(1)} %bitcast.126, f32[4096]{0:T(1024)S(1)} %bitcast.129, f32[256]{0:T(256)S(1)} %bitcast.143, f32[4096]{0:T(1024)S(1)} %bitcast.128, f32[256]{0:T(256)S(1)} %bitcast.142, f32[4096]{0:T(1024)S(1)} %bitcast.130, f32[256]{0:T(256)S(1)} %bitcast.141, ...), kind=kLoop, calls=%fused_computation.61.clone.1 | loop fusion | flops 46136576 | bytes 104448 | tf_op jit(solution)/shard_map/while/body/eval_jaxpr/reduce_sum | solution.py:76
  365.8 0.1 copy.97
  365.9 10.8 %gather_fusion.1 = f32[4096,6]{1,0:T(8,128)S(1)} fusion(f32[6,320]{0,1:T(8,128)S(1)} %copy.97, s32[4096]{0:T(1024)S(1)} %broadcast_clamp_fusion), kind=kCustom, calls=%fused_computation.1.clone | custom fusion | bytes 212992 | tf_op jit(solution)/shard_map/jit(_take)/gather | solution.py:125
  376.7 0.7 select_bitcast_fusion
  377.4 1.7 multiply_reduce_fusion.1
  379.2 0.7 multiply_reduce_fusion
  380.0 0.6 multiply_reduce_fusion.4
  380.6 22.3 %all-reduce = (f32[]{:T(128)}, f32[]{:T(128)}, f32[]{:T(128)}) all-reduce(f32[]{:T(128)} %get-tuple-element.191, f32[]{:T(128)} %get-tuple-element.190, f32[]{:T(128)} %get-tuple-element.189), channel_id=1, replica_groups=mesh['groups'=2,'blk_0'=16,'blk_1'=4,'blk_2'=2] {'blk_0'}, use_global_device_ids=true, to_apply=%region_29.31 | all-reduce | flops 3 | bytes 24 | tf_op jit(solution)/shard_map/psum | solution.py:54
  402.8 6.7 %all-reduce.2 = (f32[]{:T(128)}, f32[]{:T(128)}, f32[]{:T(128)}) all-reduce(f32[]{:T(128)} %get-tuple-element.214, f32[]{:T(128)} %get-tuple-element.215, f32[]{:T(128)} %get-tuple-element.216), channel_id=1, replica_groups=mesh['groups'=2,'blk_0'=16,'blk_1'=4,'blk_2'=2] {'blk_1'}, use_global_device_ids=true, to_apply=%region_30.32 | all-reduce | flops 3 | bytes 24 | tf_op jit(solution)/shard_map/psum | solution.py:54
  409.5 12.4 %all-reduce.4 = (f32[]{:T(128)}, f32[]{:T(128)}, f32[]{:T(128)}) all-reduce(f32[]{:T(128)} %get-tuple-element.219, f32[]{:T(128)} %get-tuple-element.220, f32[]{:T(128)} %get-tuple-element.221), channel_id=1, replica_groups=mesh['groups'=2,'blk_0'=16,'blk_1'=4,'blk_2'=2] {'blk_2'}, use_global_device_ids=true, to_apply=%region_31.33 | all-reduce | flops 3 | bytes 24 | tf_op jit(solution)/shard_map/psum | solution.py:54
  428.1 0.6 multiply_add_fusion
  428.7 0.6 multiply_subtract_fusion
  (86 shorter events, 3.6 us)
Async XLA Ops:
  69.8 118.7 %collective-permute-start = (f32[6,32]{1,0:T(8,128)S(1)}, f32[6,32]{1,0:T(8,128)S(1)}, u32[]{:S(2)}, u32[]{:S(2)}) collective-permute-start(f32[6,32]{1,0:T(8,128)S(1)} %get-tuple-element.261), channel_id=1, source_target_pairs={{0,1},{1,2},{2,3},{3,4},{4,5},{5,6},{6,7},{7,8},{8,9},{9,10},{10,1... | collective-permute-start | bytes 2312 | tf_op jit(solution)/shard_map/ppermute | solution.py:24
  69.9 118.6 %collective-permute-start.1 = (f32[6,32]{1,0:T(8,128)S(1)}, f32[6,32]{1,0:T(8,128)S(1)}, u32[]{:S(2)}, u32[]{:S(2)}) collective-permute-start(f32[6,32]{1,0:T(8,128)S(1)} %get-tuple-element.262), channel_id=1, source_target_pairs={{1,0},{2,1},{3,2},{4,3},{5,4},{6,5},{7,6},{8,7},{9,8},{10,9},{11,1... | collective-permute-start | bytes 2312 | tf_op jit(solution)/shard_map/ppermute | solution.py:26
  121.3 0.7 copy-start
  122.1 66.1 %copy-start.2 = (s32[16,256]{1,0:T(8,128)S(1)}, s32[16,256]{1,0:T(8,128)}, u32[]{:S(2)}) copy-start(s32[16,256]{1,0:T(8,128)} %param.12) | copy-start | bytes 49156
  200.3 1.8 copy-start.3
  202.0 0.8 copy-start.1
  247.6 118.1 %collective-permute-start.2 = (f32[6,32]{1,0:T(8,128)S(1)}, f32[6,32]{1,0:T(8,128)S(1)}, u32[]{:S(2)}, u32[]{:S(2)}) collective-permute-start(f32[6,32]{1,0:T(8,128)S(1)} %get-tuple-element.259), channel_id=1, source_target_pairs={{0,1},{1,2},{2,3},{3,4},{4,5},{5,6},{6,7},{7,8},{8,9},{9,10},{10,1... | collective-permute-start | bytes 2312 | tf_op jit(solution)/shard_map/ppermute | solution.py:24
  249.5 116.2 %collective-permute-start.3 = (f32[6,32]{1,0:T(8,128)S(1)}, f32[6,32]{1,0:T(8,128)S(1)}, u32[]{:S(2)}, u32[]{:S(2)}) collective-permute-start(f32[6,32]{1,0:T(8,128)S(1)} %get-tuple-element.260), channel_id=1, source_target_pairs={{1,0},{2,1},{3,2},{4,3},{5,4},{6,5},{7,6},{8,7},{9,8},{10,9},{11,1... | collective-permute-start | bytes 2312 | tf_op jit(solution)/shard_map/ppermute | solution.py:26
where the time goes:
time: 430 us; the launch traced here: 429 us
  blocking collectives  243 us (57%)
  other arithmetic  144 us (33%)
  local copies, waits for them, and re-layouts  28.6 us (7%)
  between operations  10.7 us (2%)
    psum x9, blocking collectives, one_axis_at_a_time(): return functools.reduce(lax.psum, axes, array)  148 us
    reduce_sum x16, other arithmetic, far_tile(): out_x = jnp.sum(coef_a * col_vec[0][None, :] + weighted * dx, axis=1)  130 us
    all_gather x6, blocking collectives, stacked_from(): tiles = lax.all_gather(tiles, axes[k], axis=0, tiled=True)  94.7 us
    gather x2, local copies, waits for them, and re-layouts, on_device(): picked = jnp.take(extended, local_slot, axis=1)  21.6 us
  transfers between devices with their start and end apart: 4, of which 0 were waited for; matrix products, arithmetic and copies ran while one was open for 32% of the time, Pallas kernels for 0%

commit v1 on v0

--- a/solution.py
+++ b/solution.py
@@ -39,7 +39,9 @@
 def stacked_from(array, axes, turns):
     tiles = array[None]
     for k in turns:
-        tiles = lax.all_gather(tiles, axes[k], axis=0, tiled=True)
+        tiles = jnp.concatenate(
+            lax.all_to_all(jnp.stack([tiles] * lax.axis_size(axes[k])), axes[k], 0, 0), axis=0
+        )
     held = [lax.axis_size(axes[k]) for k in reversed(turns)]
     tiles = tiles.reshape(*held, *array.shape)
     turned = sorted(range(len(turns)), key=lambda place: turns[len(turns) - 1 - place])

time: 430 us -> 402 us (0.935)
  blocking collectives: 243 us -> 190 us
  starting transfers between devices: 2.42 us -> 18.4 us
  waiting for transfers between devices: 0.01 us -> 5.36 us
    all_gather x6 -> x0, blocking collectives: 94.7 us -> none  [stacked_from(): tiles = lax.all_gather(tiles, axes[k], axis=0, tiled=True)]
    all_to_all x0 -> x3, blocking collectives: none -> 32 us  [stacked_from(): lax.all_to_all(jnp.stack([tiles] * lax.axis_size(axes[k])), axes[k], 0, 0)]
    all_to_all x0 -> x3, starting transfers between devices: none -> 15.6 us  [stacked_from(): lax.all_to_all(jnp.stack([tiles] * lax.axis_size(axes[k])), axes[k], 0, 0)]
    psum x9, blocking collectives: 148 us -> 158 us  [one_axis_at_a_time(): return functools.reduce(lax.psum, axes, array)]
  transfers between devices with their start and end apart: 4 -> 7, of which waited for: 0 -> 2; matrix products, arithmetic and copies ran while one was open for 32% -> 8% of each run, Pallas kernels for 0% -> 0%
where the time goes in v1:
time: 402 us; the launch traced here: 401 us
  blocking collectives  190 us (47%)
  other arithmetic  145 us (36%)
  local copies, waits for them, and re-layouts  31.1 us (8%)
  starting transfers between devices  18.4 us (5%)
  between operations  10.7 us (3%)
  waiting for transfers between devices  5.36 us (1%)
    psum x9, blocking collectives, one_axis_at_a_time(): return functools.reduce(lax.psum, axes, array)  158 us
    reduce_sum x16, other arithmetic, far_tile(): out_x = jnp.sum(coef_a * col_vec[0][None, :] + weighted * dx, axis=1)  130 us
    all_to_all x3, blocking collectives, stacked_from(): lax.all_to_all(jnp.stack([tiles] * lax.axis_size(axes[k])), axes[k], 0, 0)  32 us
    gather x2, local copies, waits for them, and re-layouts, on_device(): picked = jnp.take(extended, local_slot, axis=1)  21.6 us
    all_to_all x3, starting transfers between devices, stacked_from(): lax.all_to_all(jnp.stack([tiles] * lax.axis_size(axes[k])), axes[k], 0, 0)  15.6 us
  transfers between devices with their start and end apart: 7, of which 2 were waited for; matrix products, arithmetic and copies ran while one was open for 8% of the time, Pallas kernels for 0%

profile of v1, /device:TPU:33, one launch (start us, length us, event | category | flops | bytes accessed | tf_op | source)
XLA Modules:
  0.0 401.2 jit_solution(2598114479817961360)
XLA Ops:
  0.6 1.3 multiply_reduce_fusion.9
  1.9 43.8 %psum.126 = f32[]{:T(128)} all-reduce(f32[]{:T(128)} %multiply_reduce_fusion.9), channel_id=1, replica_groups=mesh['groups'=2,'blk_0'=16,'blk_1'=4,'blk_2'=2] {'blk_0'}, use_global_device_ids=true, to_apply=%region_1.2 | all-reduce | flops 1 | bytes 8 | tf_op jit(solution)/shard_map/psum | solution.py:56
  45.7 9.5 %psum.127 = f32[]{:T(128)} all-reduce(f32[]{:T(128)} %psum.126), channel_id=1, replica_groups=mesh['groups'=2,'blk_0'=16,'blk_1'=4,'blk_2'=2] {'blk_1'}, use_global_device_ids=true, to_apply=%region_2.3 | all-reduce | flops 1 | bytes 8 | tf_op jit(solution)/shard_map/psum | solution.py:56
  55.2 12.4 %psum.128 = f32[]{:T(128)} all-reduce(f32[]{:T(128)} %psum.127), channel_id=1, replica_groups=mesh['groups'=2,'blk_0'=16,'blk_1'=4,'blk_2'=2] {'blk_2'}, use_global_device_ids=true, to_apply=%region_3.4 | all-reduce | flops 1 | bytes 8 | tf_op jit(solution)/shard_map/psum | solution.py:56
  68.4 0.7 broadcast_divide_fusion
  69.0 0.8 fusion.53
  70.4 0.7 pad_maximum_fusion.5
  71.1 0.6 stack.66
  71.7 3.3 all-to-all-start
  75.1 0.7 fusion.55
  75.8 3.4 all-to-all-done
  79.2 0.8 stack.67
  80.0 5.0 %all-to-all-start.1 = ((f32[16,4,6,256]{3,1,2,0:T(4,128)}), f32[16,4,6,256]{3,1,2,0:T(4,128)S(1)}, u32[]{:S(2)}, u32[]{:S(2)}) async-start(f32[16,4,6,256]{3,1,2,0:T(4,128)} %stack.67), calls=%async_computation.1 | async-start | bytes 786432 | tf_op jit(solution)/shard_map/all_to_all | solution.py:43
  85.0 0.7 compare_and_fusion
  85.9 0.8 copy.133
  86.8 0.8 fusion.48
  87.7 10.8 %gather_fusion = f32[4096,6]{1,0:T(8,128)S(1)} fusion(f32[6,320]{0,1:T(8,128)S(1)} %copy.134, s32[4096]{0:T(1024)S(1)} %broadcast_clamp_fusion), kind=kCustom, calls=%fused_computation.clone | custom fusion | bytes 212992 | tf_op jit(solution)/shard_map/jit(_take)/gather | solution.py:127
  98.5 0.7 select_bitcast_fusion.1
  99.2 1.7 multiply_reduce_fusion.3
  101.0 0.7 multiply_reduce_fusion.2
  102.1 11.3 %all_to_all.30 = f32[2,64,6,256]{3,1,2,0:T(8,128)S(1)} all-to-all(f32[2,64,6,256]{3,1,2,0:T(8,128)S(1)} %pad_maximum_fusion), channel_id=1, replica_groups=mesh['groups'=2,'blk_0'=16,'blk_1'=4,'blk_2'=2] {'blk_2'}, dimensions={0} | all-to-all | bytes 1572864 | tf_op jit(solution)/shard_map/all_to_all | solution.py:43
  113.3 0.6 copy.145
  114.7 0.5 copy_bitcast_fusion.2
  115.3 66.1 %while.26 = (s32[]{:T(128)}, f32[3,256]{1,0:T(4,128)S(1)}, f32[3,256]{1,0:T(4,128)S(1)}, f32[8,3,4096]{2,1,0:T(4,128)S(1)}, f32[8,3,4096]{2,1,0:T(4,128)S(1)}, /*index=5*/s32[]{:T(128)}, s32[]{:T(128)}, s32[]{}, s32[]{}) while((s32[]{:T(128)}, f32[3,256]{1,0:T(4,128)S(1)}, f32[3,256]{1,0:T(4,128)S(1)}, ...), condition=%wide.region_8.9_spmd.clone, body=%wide.region_4.0_spmd.clone.sunk | while | flops 46139652 | bytes 316555 | solution.py:95
  115.4 8.1 %fusion.65 = (f32[256]{0:T(256)S(1)}, f32[256]{0:T(256)S(1)}, f32[256]{0:T(256)S(1)}) fusion(f32[4096]{0:T(1024)S(1)} %bitcast.122, f32[4096]{0:T(1024)S(1)} %bitcast.125, f32[256]{0:T(256)S(1)} %bitcast.144, f32[4096]{0:T(1024)S(1)} %bitcast.124, f32[256]{0:T(256)S(1)} %bitcast.143, f32[4096]{0:T(1024)S(1)} %bitcast.126, f32[256]{0:T(256)S(1)} %bitcast.142, ...), kind=kLoop, calls=%fused_computation.23.clone.1 | loop fusion | flops 46136576 | bytes 104448 | tf_op jit(solution)/shard_map/while/body/eval_jaxpr/reduce_sum | solution.py:78
  123.7 8.1 %fusion.65 = (f32[256]{0:T(256)S(1)}, f32[256]{0:T(256)S(1)}, f32[256]{0:T(256)S(1)}) fusion(f32[4096]{0:T(1024)S(1)} %bitcast.122, f32[4096]{0:T(1024)S(1)} %bitcast.125, f32[256]{0:T(256)S(1)} %bitcast.144, f32[4096]{0:T(1024)S(1)} %bitcast.124, f32[256]{0:T(256)S(1)} %bitcast.143, f32[4096]{0:T(1024)S(1)} %bitcast.126, f32[256]{0:T(256)S(1)} %bitcast.142, ...), kind=kLoop, calls=%fused_computation.23.clone.1 | loop fusion | flops 46136576 | bytes 104448 | tf_op jit(solution)/shard_map/while/body/eval_jaxpr/reduce_sum | solution.py:78
  132.0 8.1 %fusion.65 = (f32[256]{0:T(256)S(1)}, f32[256]{0:T(256)S(1)}, f32[256]{0:T(256)S(1)}) fusion(f32[4096]{0:T(1024)S(1)} %bitcast.122, f32[4096]{0:T(1024)S(1)} %bitcast.125, f32[256]{0:T(256)S(1)} %bitcast.144, f32[4096]{0:T(1024)S(1)} %bitcast.124, f32[256]{0:T(256)S(1)} %bitcast.143, f32[4096]{0:T(1024)S(1)} %bitcast.126, f32[256]{0:T(256)S(1)} %bitcast.142, ...), kind=kLoop, calls=%fused_computation.23.clone.1 | loop fusion | flops 46136576 | bytes 104448 | tf_op jit(solution)/shard_map/while/body/eval_jaxpr/reduce_sum | solution.py:78
  140.2 8.1 %fusion.65 = (f32[256]{0:T(256)S(1)}, f32[256]{0:T(256)S(1)}, f32[256]{0:T(256)S(1)}) fusion(f32[4096]{0:T(1024)S(1)} %bitcast.122, f32[4096]{0:T(1024)S(1)} %bitcast.125, f32[256]{0:T(256)S(1)} %bitcast.144, f32[4096]{0:T(1024)S(1)} %bitcast.124, f32[256]{0:T(256)S(1)} %bitcast.143, f32[4096]{0:T(1024)S(1)} %bitcast.126, f32[256]{0:T(256)S(1)} %bitcast.142, ...), kind=kLoop, calls=%fused_computation.23.clone.1 | loop fusion | flops 46136576 | bytes 104448 | tf_op jit(solution)/shard_map/while/body/eval_jaxpr/reduce_sum | solution.py:78
  148.5 8.1 %fusion.65 = (f32[256]{0:T(256)S(1)}, f32[256]{0:T(256)S(1)}, f32[256]{0:T(256)S(1)}) fusion(f32[4096]{0:T(1024)S(1)} %bitcast.122, f32[4096]{0:T(1024)S(1)} %bitcast.125, f32[256]{0:T(256)S(1)} %bitcast.144, f32[4096]{0:T(1024)S(1)} %bitcast.124, f32[256]{0:T(256)S(1)} %bitcast.143, f32[4096]{0:T(1024)S(1)} %bitcast.126, f32[256]{0:T(256)S(1)} %bitcast.142, ...), kind=kLoop, calls=%fused_computation.23.clone.1 | loop fusion | flops 46136576 | bytes 104448 | tf_op jit(solution)/shard_map/while/body/eval_jaxpr/reduce_sum | solution.py:78
  156.8 8.1 %fusion.65 = (f32[256]{0:T(256)S(1)}, f32[256]{0:T(256)S(1)}, f32[256]{0:T(256)S(1)}) fusion(f32[4096]{0:T(1024)S(1)} %bitcast.122, f32[4096]{0:T(1024)S(1)} %bitcast.125, f32[256]{0:T(256)S(1)} %bitcast.144, f32[4096]{0:T(1024)S(1)} %bitcast.124, f32[256]{0:T(256)S(1)} %bitcast.143, f32[4096]{0:T(1024)S(1)} %bitcast.126, f32[256]{0:T(256)S(1)} %bitcast.142, ...), kind=kLoop, calls=%fused_computation.23.clone.1 | loop fusion | flops 46136576 | bytes 104448 | tf_op jit(solution)/shard_map/while/body/eval_jaxpr/reduce_sum | solution.py:78
  165.0 8.1 %fusion.65 = (f32[256]{0:T(256)S(1)}, f32[256]{0:T(256)S(1)}, f32[256]{0:T(256)S(1)}) fusion(f32[4096]{0:T(1024)S(1)} %bitcast.122, f32[4096]{0:T(1024)S(1)} %bitcast.125, f32[256]{0:T(256)S(1)} %bitcast.144, f32[4096]{0:T(1024)S(1)} %bitcast.124, f32[256]{0:T(256)S(1)} %bitcast.143, f32[4096]{0:T(1024)S(1)} %bitcast.126, f32[256]{0:T(256)S(1)} %bitcast.142, ...), kind=kLoop, calls=%fused_computation.23.clone.1 | loop fusion | flops 46136576 | bytes 104448 | tf_op jit(solution)/shard_map/while/body/eval_jaxpr/reduce_sum | solution.py:78
  173.3 8.1 %fusion.65 = (f32[256]{0:T(256)S(1)}, f32[256]{0:T(256)S(1)}, f32[256]{0:T(256)S(1)}) fusion(f32[4096]{0:T(1024)S(1)} %bitcast.122, f32[4096]{0:T(1024)S(1)} %bitcast.125, f32[256]{0:T(256)S(1)} %bitcast.144, f32[4096]{0:T(1024)S(1)} %bitcast.124, f32[256]{0:T(256)S(1)} %bitcast.143, f32[4096]{0:T(1024)S(1)} %bitcast.126, f32[256]{0:T(256)S(1)} %bitcast.142, ...), kind=kLoop, calls=%fused_computation.23.clone.1 | loop fusion | flops 46136576 | bytes 104448 | tf_op jit(solution)/shard_map/while/body/eval_jaxpr/reduce_sum | solution.py:78
  181.4 0.6 multiply_reduce_fusion.8
  182.0 23.2 %all-reduce.1 = (f32[]{:T(128)}, f32[]{:T(128)}) all-reduce(f32[]{:T(128)} %get-tuple-element.195, f32[]{:T(128)} %get-tuple-element.194), channel_id=1, replica_groups=mesh['groups'=2,'blk_0'=16,'blk_1'=4,'blk_2'=2] {'blk_0'}, use_global_device_ids=true, to_apply=%region_17.19 | all-reduce | flops 2 | bytes 16 | tf_op jit(solution)/shard_map/psum | solution.py:56
  205.2 7.5 %all-reduce.3 = (f32[]{:T(128)}, f32[]{:T(128)}) all-reduce(f32[]{:T(128)} %get-tuple-element.219, f32[]{:T(128)} %get-tuple-element.220), channel_id=1, replica_groups=mesh['groups'=2,'blk_0'=16,'blk_1'=4,'blk_2'=2] {'blk_1'}, use_global_device_ids=true, to_apply=%region_18.20 | all-reduce | flops 2 | bytes 16 | tf_op jit(solution)/shard_map/psum | solution.py:56
  212.7 12.3 %all-reduce.5 = (f32[]{:T(128)}, f32[]{:T(128)}) all-reduce(f32[]{:T(128)} %get-tuple-element.224, f32[]{:T(128)} %get-tuple-element.225), channel_id=1, replica_groups=mesh['groups'=2,'blk_0'=16,'blk_1'=4,'blk_2'=2] {'blk_2'}, use_global_device_ids=true, to_apply=%region_19.21 | all-reduce | flops 2 | bytes 16 | tf_op jit(solution)/shard_map/psum | solution.py:56
  227.0 0.7 subtract_divide_fusion
  227.7 6.6 %all_to_all.31 = f32[4,1,6,256]{3,1,2,0:T(1,128)S(1)} all-to-all(f32[4,1,6,256]{3,1,2,0:T(1,128)S(1)} %stack.69), channel_id=1, replica_groups=mesh['groups'=2,'blk_0'=16,'blk_1'=4,'blk_2'=2] {'blk_1'}, dimensions={0} | all-to-all | bytes 49152 | tf_op jit(solution)/shard_map/all_to_all | solution.py:43
  234.3 0.8 stack.70
  235.1 7.3 %all-to-all-start.4 = ((f32[16,4,6,256]{3,1,2,0:T(4,128)}), f32[16,4,6,256]{3,1,2,0:T(4,128)S(1)}, u32[]{:S(2)}, u32[]{:S(2)}) async-start(f32[16,4,6,256]{3,1,2,0:T(4,128)} %stack.70), calls=%async_computation.4 | async-start | bytes 786432 | tf_op jit(solution)/shard_map/all_to_all | solution.py:43
  242.5 2.0 collective-permute-start.2
  245.6 2.0 collective-permute-done.3
  247.8 10.8 %gather_fusion.1 = f32[4096,6]{1,0:T(8,128)S(1)} fusion(f32[6,320]{0,1:T(8,128)S(1)} %copy.142, s32[4096]{0:T(1024)S(1)} %broadcast_clamp_fusion), kind=kCustom, calls=%fused_computation.1.clone | custom fusion | bytes 212992 | tf_op jit(solution)/shard_map/jit(_take)/gather | solution.py:127
  258.5 0.7 select_bitcast_fusion
  259.3 1.7 multiply_reduce_fusion.1
  261.0 0.7 multiply_reduce_fusion
  262.1 14.1 %all_to_all.32 = f32[2,64,6,256]{3,1,2,0:T(8,128)S(1)} all-to-all(f32[2,64,6,256]{3,1,2,0:T(8,128)S(1)} %pad_maximum_fusion.1), channel_id=1, replica_groups=mesh['groups'=2,'blk_0'=16,'blk_1'=4,'blk_2'=2] {'blk_2'}, dimensions={0} | all-to-all | bytes 1572864 | tf_op jit(solution)/shard_map/all_to_all | solution.py:43
  276.2 0.6 copy.146
  276.8 0.5 reshape.144
  278.2 66.1 %while.27 = (s32[]{:T(128)}, f32[3,256]{1,0:T(4,128)S(1)}, f32[3,256]{1,0:T(4,128)S(1)}, f32[8,3,4096]{2,1,0:T(4,128)S(1)}, f32[8,3,4096]{2,1,0:T(4,128)S(1)}, /*index=5*/s32[]{:T(128)}, s32[]{:T(128)}, s32[]{}, s32[]{}) while((s32[]{:T(128)}, f32[3,256]{1,0:T(4,128)S(1)}, f32[3,256]{1,0:T(4,128)S(1)}, ...), condition=%wide.region_24.26_spmd.clone, body=%wide.region_20.25_spmd.clone.sunk | while | flops 46139652 | bytes 316555 | solution.py:95
  278.3 8.1 %fusion.67 = (f32[256]{0:T(256)S(1)}, f32[256]{0:T(256)S(1)}, f32[256]{0:T(256)S(1)}) fusion(f32[4096]{0:T(1024)S(1)} %bitcast.128, f32[4096]{0:T(1024)S(1)} %bitcast.131, f32[256]{0:T(256)S(1)} %bitcast.147, f32[4096]{0:T(1024)S(1)} %bitcast.130, f32[256]{0:T(256)S(1)} %bitcast.146, f32[4096]{0:T(1024)S(1)} %bitcast.132, f32[256]{0:T(256)S(1)} %bitcast.145, ...), kind=kLoop, calls=%fused_computation.61.clone.1 | loop fusion | flops 46136576 | bytes 104448 | tf_op jit(solution)/shard_map/while/body/eval_jaxpr/reduce_sum | solution.py:78
  286.6 8.1 %fusion.67 = (f32[256]{0:T(256)S(1)}, f32[256]{0:T(256)S(1)}, f32[256]{0:T(256)S(1)}) fusion(f32[4096]{0:T(1024)S(1)} %bitcast.128, f32[4096]{0:T(1024)S(1)} %bitcast.131, f32[256]{0:T(256)S(1)} %bitcast.147, f32[4096]{0:T(1024)S(1)} %bitcast.130, f32[256]{0:T(256)S(1)} %bitcast.146, f32[4096]{0:T(1024)S(1)} %bitcast.132, f32[256]{0:T(256)S(1)} %bitcast.145, ...), kind=kLoop, calls=%fused_computation.61.clone.1 | loop fusion | flops 46136576 | bytes 104448 | tf_op jit(solution)/shard_map/while/body/eval_jaxpr/reduce_sum | solution.py:78
  294.8 8.1 %fusion.67 = (f32[256]{0:T(256)S(1)}, f32[256]{0:T(256)S(1)}, f32[256]{0:T(256)S(1)}) fusion(f32[4096]{0:T(1024)S(1)} %bitcast.128, f32[4096]{0:T(1024)S(1)} %bitcast.131, f32[256]{0:T(256)S(1)} %bitcast.147, f32[4096]{0:T(1024)S(1)} %bitcast.130, f32[256]{0:T(256)S(1)} %bitcast.146, f32[4096]{0:T(1024)S(1)} %bitcast.132, f32[256]{0:T(256)S(1)} %bitcast.145, ...), kind=kLoop, calls=%fused_computation.61.clone.1 | loop fusion | flops 46136576 | bytes 104448 | tf_op jit(solution)/shard_map/while/body/eval_jaxpr/reduce_sum | solution.py:78
  303.1 8.1 %fusion.67 = (f32[256]{0:T(256)S(1)}, f32[256]{0:T(256)S(1)}, f32[256]{0:T(256)S(1)}) fusion(f32[4096]{0:T(1024)S(1)} %bitcast.128, f32[4096]{0:T(1024)S(1)} %bitcast.131, f32[256]{0:T(256)S(1)} %bitcast.147, f32[4096]{0:T(1024)S(1)} %bitcast.130, f32[256]{0:T(256)S(1)} %bitcast.146, f32[4096]{0:T(1024)S(1)} %bitcast.132, f32[256]{0:T(256)S(1)} %bitcast.145, ...), kind=kLoop, calls=%fused_computation.61.clone.1 | loop fusion | flops 46136576 | bytes 104448 | tf_op jit(solution)/shard_map/while/body/eval_jaxpr/reduce_sum | solution.py:78
  311.4 8.1 %fusion.67 = (f32[256]{0:T(256)S(1)}, f32[256]{0:T(256)S(1)}, f32[256]{0:T(256)S(1)}) fusion(f32[4096]{0:T(1024)S(1)} %bitcast.128, f32[4096]{0:T(1024)S(1)} %bitcast.131, f32[256]{0:T(256)S(1)} %bitcast.147, f32[4096]{0:T(1024)S(1)} %bitcast.130, f32[256]{0:T(256)S(1)} %bitcast.146, f32[4096]{0:T(1024)S(1)} %bitcast.132, f32[256]{0:T(256)S(1)} %bitcast.145, ...), kind=kLoop, calls=%fused_computation.61.clone.1 | loop fusion | flops 46136576 | bytes 104448 | tf_op jit(solution)/shard_map/while/body/eval_jaxpr/reduce_sum | solution.py:78
  319.6 8.1 %fusion.67 = (f32[256]{0:T(256)S(1)}, f32[256]{0:T(256)S(1)}, f32[256]{0:T(256)S(1)}) fusion(f32[4096]{0:T(1024)S(1)} %bitcast.128, f32[4096]{0:T(1024)S(1)} %bitcast.131, f32[256]{0:T(256)S(1)} %bitcast.147, f32[4096]{0:T(1024)S(1)} %bitcast.130, f32[256]{0:T(256)S(1)} %bitcast.146, f32[4096]{0:T(1024)S(1)} %bitcast.132, f32[256]{0:T(256)S(1)} %bitcast.145, ...), kind=kLoop, calls=%fused_computation.61.clone.1 | loop fusion | flops 46136576 | bytes 104448 | tf_op jit(solution)/shard_map/while/body/eval_jaxpr/reduce_sum | solution.py:78
  327.9 8.1 %fusion.67 = (f32[256]{0:T(256)S(1)}, f32[256]{0:T(256)S(1)}, f32[256]{0:T(256)S(1)}) fusion(f32[4096]{0:T(1024)S(1)} %bitcast.128, f32[4096]{0:T(1024)S(1)} %bitcast.131, f32[256]{0:T(256)S(1)} %bitcast.147, f32[4096]{0:T(1024)S(1)} %bitcast.130, f32[256]{0:T(256)S(1)} %bitcast.146, f32[4096]{0:T(1024)S(1)} %bitcast.132, f32[256]{0:T(256)S(1)} %bitcast.145, ...), kind=kLoop, calls=%fused_computation.61.clone.1 | loop fusion | flops 46136576 | bytes 104448 | tf_op jit(solution)/shard_map/while/body/eval_jaxpr/reduce_sum | solution.py:78
  336.1 8.1 %fusion.67 = (f32[256]{0:T(256)S(1)}, f32[256]{0:T(256)S(1)}, f32[256]{0:T(256)S(1)}) fusion(f32[4096]{0:T(1024)S(1)} %bitcast.128, f32[4096]{0:T(1024)S(1)} %bitcast.131, f32[256]{0:T(256)S(1)} %bitcast.147, f32[4096]{0:T(1024)S(1)} %bitcast.130, f32[256]{0:T(256)S(1)} %bitcast.146, f32[4096]{0:T(1024)S(1)} %bitcast.132, f32[256]{0:T(256)S(1)} %bitcast.145, ...), kind=kLoop, calls=%fused_computation.61.clone.1 | loop fusion | flops 46136576 | bytes 104448 | tf_op jit(solution)/shard_map/while/body/eval_jaxpr/reduce_sum | solution.py:78
  344.3 0.6 multiply_reduce_fusion.4
  344.9 26.6 %all-reduce = (f32[]{:T(128)}, f32[]{:T(128)}, f32[]{:T(128)}) all-reduce(f32[]{:T(128)} %get-tuple-element.193, f32[]{:T(128)} %get-tuple-element.192, f32[]{:T(128)} %get-tuple-element.191), channel_id=1, replica_groups=mesh['groups'=2,'blk_0'=16,'blk_1'=4,'blk_2'=2] {'blk_0'}, use_global_device_ids=true, to_apply=%region_29.31 | all-reduce | flops 3 | bytes 24 | tf_op jit(solution)/shard_map/psum | solution.py:56
  371.4 10.3 %all-reduce.2 = (f32[]{:T(128)}, f32[]{:T(128)}, f32[]{:T(128)}) all-reduce(f32[]{:T(128)} %get-tuple-element.216, f32[]{:T(128)} %get-tuple-element.217, f32[]{:T(128)} %get-tuple-element.218), channel_id=1, replica_groups=mesh['groups'=2,'blk_0'=16,'blk_1'=4,'blk_2'=2] {'blk_1'}, use_global_device_ids=true, to_apply=%region_30.32 | all-reduce | flops 3 | bytes 24 | tf_op jit(solution)/shard_map/psum | solution.py:56
  381.8 12.1 %all-reduce.4 = (f32[]{:T(128)}, f32[]{:T(128)}, f32[]{:T(128)}) all-reduce(f32[]{:T(128)} %get-tuple-element.221, f32[]{:T(128)} %get-tuple-element.222, f32[]{:T(128)} %get-tuple-element.223), channel_id=1, replica_groups=mesh['groups'=2,'blk_0'=16,'blk_1'=4,'blk_2'=2] {'blk_2'}, use_global_device_ids=true, to_apply=%region_31.33 | all-reduce | flops 3 | bytes 24 | tf_op jit(solution)/shard_map/psum | solution.py:56
  400.0 0.6 multiply_add_fusion
  400.6 0.6 multiply_subtract_fusion
  (95 shorter events, 5.7 us)
Async XLA Ops:
  69.8 16.9 %collective-permute-start = (f32[6,32]{1,0:T(8,128)S(1)}, f32[6,32]{1,0:T(8,128)S(1)}, u32[]{:S(2)}, u32[]{:S(2)}) collective-permute-start(f32[6,32]{1,0:T(8,128)S(1)} %get-tuple-element.263), channel_id=1, source_target_pairs={{0,1},{1,2},{2,3},{3,4},{4,5},{5,6},{6,7},{7,8},{8,9},{9,10},{10,1... | collective-permute-start | bytes 2312 | tf_op jit(solution)/shard_map/ppermute | solution.py:24
  69.9 16.9 %collective-permute-start.1 = (f32[6,32]{1,0:T(8,128)S(1)}, f32[6,32]{1,0:T(8,128)S(1)}, u32[]{:S(2)}, u32[]{:S(2)}) collective-permute-start(f32[6,32]{1,0:T(8,128)S(1)} %get-tuple-element.264), channel_id=1, source_target_pairs={{1,0},{2,1},{3,2},{4,3},{5,4},{6,5},{7,6},{8,7},{9,8},{10,9},{11,1... | collective-permute-start | bytes 2312 | tf_op jit(solution)/shard_map/ppermute | solution.py:26
  71.7 7.5 %all-to-all-start = ((f32[4,1,6,256]{3,1,2,0:T(1,128)}), f32[4,1,6,256]{3,1,2,0:T(1,128)S(1)}, u32[]{:S(2)}, u32[]{:S(2)}) async-start(f32[4,1,6,256]{3,1,2,0:T(1,128)} %stack.66), calls=%async_computation | async-start | bytes 49152 | tf_op jit(solution)/shard_map/all_to_all | solution.py:43
  80.0 21.8 %all-to-all-start.1 = ((f32[16,4,6,256]{3,1,2,0:T(4,128)}), f32[16,4,6,256]{3,1,2,0:T(4,128)S(1)}, u32[]{:S(2)}, u32[]{:S(2)}) async-start(f32[16,4,6,256]{3,1,2,0:T(4,128)} %stack.67), calls=%async_computation.1 | async-start | bytes 786432 | tf_op jit(solution)/shard_map/all_to_all | solution.py:43
  99.2 1.7 copy-start.2
  114.6 0.7 copy-start
  115.3 66.1 %copy-start.1 = (f32[3,256]{1,0:T(4,128)S(1)}, f32[3,256]{1,0:T(4,128)}, u32[]{:S(2)}) copy-start(f32[3,256]{1,0:T(4,128)} %param.11) | copy-start | bytes 9220
  235.1 26.7 %all-to-all-start.4 = ((f32[16,4,6,256]{3,1,2,0:T(4,128)}), f32[16,4,6,256]{3,1,2,0:T(4,128)S(1)}, u32[]{:S(2)}, u32[]{:S(2)}) async-start(f32[16,4,6,256]{3,1,2,0:T(4,128)} %stack.70), calls=%async_computation.4 | async-start | bytes 786432 | tf_op jit(solution)/shard_map/all_to_all | solution.py:43
  242.5 3.1 collective-permute-start.2
  244.5 3.0 collective-permute-start.3
